TPU v7x, 128 devices: a whole 4x4x4 slice. The times are simulated.
128 devices in a mesh: seq: 64 (over z, y, x), tp: 2 (over core).
Axes of the slice: x: 4, y: 4, z: 4, core: 2. Of those that a mesh axis runs over, the one named last changes fastest.
Arguments:
- patches: bfloat16 [16384, 1280], P('seq'), may hold values from -60 to 60
- merge_up: bfloat16 [5120, 2560], P(None, 'tp'), may hold values from -0.078125 to 0.078125
- merge_down: bfloat16 [2560, 3584], P('tp'), may hold values from -0.125 to 0.125
- dest: int32 [4096], P('seq'), may hold values from 0 to 63, as said below
- slot: int32 [4096], P('seq'), may hold values from 0 to 255, as said below
- text: bfloat16 [16384, 3584], P('seq'), may hold values from -60 to 60
- positions: int32 [3, 16384], P(None, 'seq'), may hold values from 0 to 1023
- documents: int32 [16384], P('seq'), may hold values from 0 to 7, never falling along the last dimension, each value on 1 to 8448 neighbouring positions
- w_query: bfloat16 [3584, 1792], P('seq', 'tp'), may hold values from -8 to 8
- w_key: bfloat16 [3584, 256], P('seq', 'tp'), may hold values from -8 to 8
- w_value: bfloat16 [3584, 256], P('seq', 'tp'), may hold values from -0.09375 to 0.09375
Outputs:
- layer_input: bfloat16 [16384, 3584], P('seq', 'tp')
- attended: bfloat16 [16384, 1792], P('seq', 'tp')
Inputs may be any that keep to these rules, and one draw needn't show every extreme that they name: `dest`: the rows of one device name each sequence shard at most 2 times, and in every draw some sequence shard is named 2 times by the rows of every device. `slot`: no two image rows share both a sequence shard and a position. `documents`: document numbers never fall along the tokens.
All inputs are finite; a program needn't handle non-finite values.
Results may differ from a plain program's by a relative error of at most 0.0065.
Values may be sent and summed in bfloat16 or wider, within the bound.
A program may use at most 128 MiB of HBM per device.

v0:
```python
import functools

import jax
import jax.numpy as jnp
from jax import lax
from jax.experimental import pallas as pl
from jax.experimental.pallas import tpu as pltpu
from jax.sharding import PartitionSpec as P

HEAD = 128
EPS = 1e-06
THETA = 1000000.0
MASKED = -1e30
MESH = pl.DeviceIdType.MESH
F32 = jnp.float32
BF16 = jnp.bfloat16
WINDOW = 33
UNIT = 1536
EXPONENT = HEAD**-0.5 * 1.4426950408889634


def coords():
    seq = lax.axis_index("seq")
    return (seq // 16, (seq // 4) % 4, seq % 4), lax.axis_index("tp"), seq


def device(zyx, tp):
    return (zyx[0] * 16 + zyx[1] * 4 + zyx[2], tp)


def moved(zyx, dim, by):
    out = list(zyx)
    out[dim] = lax.rem(out[dim] + by + 4, 4)
    return tuple(out)


class Gather:
    ORDERS = ((2, 1, 0), (1, 0, 2), (0, 2, 1))

    def __init__(self, weights, send, recv, zyx, tp):
        self.weights, self.send, self.recv, self.zyx, self.tp = weights, send, recv, zyx, tp

    def block(self, part, phase, at, half, early):
        order = self.ORDERS[part]
        index = [None, None, None]
        for place, dim in enumerate(order):
            if place < phase:
                index[dim] = pl.ds(0, 4)
            elif place == phase:
                index[dim] = at
            else:
                index[dim] = self.zyx[dim]
        if phase:
            index[order[phase - 1]] = pl.ds(2 * half, 2)
        columns = pl.ds(384 * part, 384)
        if phase == 2 and part < 2:
            columns = pl.ds(384 * part + 256, 128) if early else pl.ds(384 * part, 256)
        return self.weights.at[index[0], index[1], index[2], :, columns]

    def copy(self, part, phase, kind, incoming=False, early=False):
        dim = self.ORDERS[part][phase]
        me = self.zyx[dim]
        back, half = ((0, 0), (0, 1), (1, 0), (0, 1), (0, 0), (1, 1))[kind]
        step = 1 if kind < 3 else -1
        if phase == 0 and kind == 2:
            back, step = 0, 2
        shift = (1 if kind < 3 else -1) * back + (step if incoming else 0)
        at = lax.rem(me - shift + 4, 4)
        ref = self.block(part, phase, at, half, early)
        sem = 54 + part * 6 + kind if early else (part * 3 + phase) * 6 + kind
        return pltpu.make_async_remote_copy(
            src_ref=ref,
            dst_ref=ref,
            send_sem=self.send.at[sem],
            recv_sem=self.recv.at[sem],
            device_id=device(moved(self.zyx, dim, step), self.tp),
            device_id_type=MESH,
        )

    def start(self, phase, parts=(0, 1, 2), early=False):
        for kind in (0, 3, 2) if phase == 0 else (0, 3, 1, 4):
            for part in parts:
                self.copy(part, phase, kind, early=early).start()

    def forward(self, phase, parts=(0, 1, 2), early=False):
        for kind in (2, 5):
            for part in parts:
                self.copy(part, phase, kind - 2, True, early).wait_recv()
                self.copy(part, phase, kind, early=early).start()

    def finish(self, phase, parts=(0, 1, 2), early=False):
        for part in parts:
            for kind in (0, 3, 2) if phase == 0 else (1, 4, 2, 5):
                self.copy(part, phase, kind, True, early).wait_recv()

    def drain(self):
        for phase in range(3):
            for part in range(3):
                for kind in (0, 3, 2) if phase == 0 else range(6):
                    self.copy(part, phase, kind).wait_send()
        for part in range(2):
            for kind in range(6):
                self.copy(part, 2, kind, early=True).wait_send()


class Ring:
    PARTS = ((0, 48), (48, 96), (144, 112))
    ORDERS = ((2, 1, 0), (1, 0, 2), (0, 2, 1))

    def __init__(self, kv, extra, send, recv, zyx, tp, seq):
        self.kv, self.extra, self.send, self.recv = kv, extra, send, recv
        self.flat = kv.reshape(16, 4, 256, 256)
        self.zyx, self.tp, self.seq = zyx, tp, seq
        z, y, x = zyx
        self.row = 4 * z + y
        self.gives_extra = (x == 3) & (self.row < 7)
        self.takes_extra = (x == 0) & (self.row > 8)

    def base(self, source, target):
        later = (target - source + 3) // 4
        return jnp.maximum(self.zyx[0] - 2 + later, 0)

    def block(self, part, phase, at, kind):
        z, y, x = self.zyx
        tokens = pl.ds(*self.PARTS[part])
        half = (0, 1, 0, 1, 0, 1)[kind]
        if phase == 0:
            index = [z, y, x]
            index[self.ORDERS[part][0]] = at
            return self.kv.at[index[0], index[1], index[2], tokens]
        if part == 0:
            two = pl.ds(2 * half, 2)
            if phase == 1:
                return self.kv.at[z, at, two, tokens]
            return self.kv.at[at, two, :, tokens]
        if part == 1:
            if phase == 1:
                return self.kv.at[at, pl.ds(2 * half, 2), x, tokens]
            base = jnp.maximum(self.row - 8, 0)
            return self.flat.at[pl.ds(base + 5 * half, 5 - half), at, tokens]
        if phase == 1:
            base = jnp.maximum(z - 2, 0)
            return self.kv.at[pl.ds(base + 2 * half, 2 - half), y, at, tokens]
        raise NotImplementedError

    def copy(self, part, phase, kind, incoming=False):
        dim = self.ORDERS[part][phase]
        me = self.zyx[dim]
        sign = 1 if kind < 3 else -1
        back = 1 if kind in (2, 5) else 0
        if phase == 0 and kind == 2:
            sign, back = 2, 0
        at = lax.rem(me - sign * (back + (1 if incoming else 0)) + 4, 4)
        if part == 2 and phase == 2:
            to = me if incoming else lax.rem(me + sign + 4, 4)
            base = self.base(at, to)
            planes = pl.ds(base, 2)
            if back:
                planes = pl.ds(base + (1 if kind == 2 else 0), 1)
            ref = self.kv.at[planes, at, :, pl.ds(*self.PARTS[2])]
        else:
            ref = self.block(part, phase, at, kind)
        sem = (part * 3 + phase) * 6 + kind
        return pltpu.make_async_remote_copy(
            src_ref=ref,
            dst_ref=ref,
            send_sem=self.send.at[sem],
            recv_sem=self.recv.at[sem],
            device_id=device(moved(self.zyx, dim, sign), self.tp),
            device_id_type=MESH,
        )

    def own_kinds(self, part, phase):
        if phase == 0:
            return (0, 3, 2)
        if (part, phase) == (2, 2):
            return (0, 3)
        if (part, phase) == (0, 2):
            return (0, 3, 1)
        return (0, 3, 1, 4)

    def sent_on(self, phase):
        return () if phase == 0 else (2, 5)

    def start(self, phase):
        for place in range(4):
            for part in range(3):
                kinds = self.own_kinds(part, phase)
                if place < len(kinds):
                    self.copy(part, phase, kinds[place]).start()
        if phase == 2:

            @pl.when(self.gives_extra)
            def _():
                self.extra_copy(False).start()

    def wait(self, *which):
        for part, phase, kind in which:
            self.copy(part, phase, kind, True).wait_recv()

    def forward(self, phase, parts=(0, 1, 2)):
        for kind in self.sent_on(phase):
            for part in parts:
                self.wait((part, phase, kind - 2))
                self.copy(part, phase, kind).start()

    def finish(self, phase):
        for part in range(3):
            for kind in self.own_kinds(part, phase) + self.sent_on(phase):
                if phase == 0 or kind not in (0, 3):
                    self.wait((part, phase, kind))

    def drain(self):
        for phase in range(3):
            for part in range(3):
                for kind in self.own_kinds(part, phase) + self.sent_on(phase):
                    self.copy(part, phase, kind).wait_send()

        @pl.when(self.gives_extra)
        def _():
            self.extra_copy(False).wait_send()

    def extra_copy(self, incoming):
        z, y, x = self.zyx
        other = (self.seq + 64 - WINDOW if incoming else self.seq + WINDOW) % 64
        sem = 54
        return pltpu.make_async_remote_copy(
            src_ref=self.kv.at[z, y, x],
            dst_ref=self.extra,
            send_sem=self.send.at[sem],
            recv_sem=self.recv.at[sem],
            device_id=(other, self.tp),
            device_id_type=MESH,
        )

    def greet(self, barrier):
        @pl.when(self.takes_extra)
        def _():
            pl.semaphore_signal(
                barrier, inc=1, device_id=(self.seq - WINDOW, self.tp), device_id_type=MESH
            )

    def greeted(self, barrier, partners):
        @pl.when(self.gives_extra)
        def _():
            pl.semaphore_wait(barrier, partners + 1)

        @pl.when(jnp.logical_not(self.gives_extra))
        def _():
            pl.semaphore_wait(barrier, partners)

    def shard(self, part, row, col):
        begin, size = self.PARTS[part]
        return (jnp.maximum(row, 0), col, begin), (row * 4 + col) * 256 + begin, size

    def row_keys(self, at):
        return [self.shard(1, self.row - 8 + r, at) for r in range(9)]

    def plane_keys(self, at):
        y = self.zyx[1]
        own = at is y
        base = jnp.maximum(self.zyx[0] - 2, 0) if own else self.base(at, y)
        planes = range(3 if own else 2)
        return [self.shard(2, (base + p) * 4 + at, col) for p in planes for col in range(4)]

    def before_keys(self):
        z = self.zyx[0]
        return [self.shard(0, 4 * z - 4 + r, col) for r in range(4) for col in range(4)]

    def edge_keys(self):
        y = self.zyx[1]
        rows = [self.row - 8 + r + 4 * ((y + r) // 4) for r in range(5)]
        return [self.shard(0, row, col) for row in rows for col in range(4)]

    def units(self):
        z, y, x = self.zyx
        left, right = lax.rem(x + 3, 4), lax.rem(x + 1, 4)
        below, above = lax.rem(y + 3, 4), lax.rem(y + 1, 4)
        before = self.before_keys()
        stream = self.row_keys(x) + self.plane_keys(y) + before[:8] + self.row_keys(left)
        stream += self.row_keys(right) + before[8:] + self.plane_keys(below)
        stream += self.plane_keys(above) + self.row_keys(lax.rem(x + 2, 4))
        stream += self.plane_keys(lax.rem(y + 2, 4)) + self.edge_keys()
        out, room = [[]], UNIT
        for (row, col, begin), at, size in stream:
            done = 0
            while done < size:
                if room == 0:
                    out.append([])
                    room = UNIT
                take = min(size - done, room)
                out[-1].append(((row, col, begin + done), at + done, take))
                done += take
                room -= take
        return out


def iota(shape, dim):
    return lax.broadcasted_iota(jnp.int32, shape, dim)


def to_column(row):
    n = row.shape[1]
    eye = iota((n, n), 0) == iota((n, n), 1)
    return jnp.sum(jnp.where(eye, jnp.broadcast_to(row, (n, n)), 0.0), axis=1, keepdims=True)


def to_row(column):
    n = column.shape[0]
    eye = iota((n, n), 0) == iota((n, n), 1)
    return jnp.sum(jnp.where(eye, jnp.broadcast_to(column, (n, n)), 0.0), axis=0, keepdims=True)


def one_hot(flag):
    return jnp.where(flag, 1.0, 0.0).astype(BF16)


def dot(a, b):
    return jnp.dot(a, b, preferred_element_type=F32)


def whole(
    patches, merge_up, merge_down, dest, slot, text, positions, documents, w_query, w_key, w_value,
    layer_out, attended_out,
    patch_v, up_v, down_v, text_v, pn, acc, disp, stage1, turned, stage2, part_f, part_s, part_r,
    merged, normed, weights, qkv, kv, extra, bounds, query, hold, top, unit_k, unit_v,
    load, send, recv, send1, recv1, send2, recv2, send3, recv3, kv_send, kv_recv,
):
    zyx, tp, seq = coords()
    z, y, x = zyx
    own = weights.at[z, y, x]
    def columns(source, begin, size, target, sem):
        return pltpu.make_async_copy(
            source.at[:, pl.ds(begin, size)], own.at[:, pl.ds(target, size)], load.at[sem]
        )

    loads = [
        columns(w_query, 0, 256, 0, 0),
        columns(w_key, 0, 128, 256, 1),
        columns(w_query, 256, 256, 384, 2),
        pltpu.make_async_copy(patches, patch_v, load.at[3]),
    ]
    own_loads = [columns(w_value, 0, 128, 640, 11), columns(w_query, 512, 384, 768, 12)]
    own_loads += loads[:3]

    def up_part(p):
        return pltpu.make_async_copy(
            merge_up.at[pl.ds(1280 * p, 1280)], up_v.at[p], load.at[4 + p]
        )

    loads += [up_part(p) for p in range(4)]
    loads.append(pltpu.make_async_copy(merge_down, down_v, load.at[8]))
    loads.append(pltpu.make_async_copy(text, text_v, load.at[9]))
    for copy in own_loads + loads[3:]:
        copy.start()

    barrier = pltpu.get_barrier_semaphore()
    partners = []
    for g in range(1, 16):
        partners.append(device(moved(moved(zyx, 0, g // 4), 1, g % 4), tp))
    for g in range(1, 4):
        partners.append(device(moved(zyx, 2, g), tp))
    partners.append((seq, 1 - tp))
    for partner in partners:
        pl.semaphore_signal(barrier, inc=1, device_id=partner, device_id_type=MESH)
    ring = Ring(kv, extra, kv_send, kv_recv, zyx, tp, seq)
    ring.greet(barrier)
    for copy in own_loads:
        copy.wait()
    ring.greeted(barrier, len(partners))

    gather = Gather(weights, send, recv, zyx, tp)
    gather.start(0)

    loads[3].wait()
    rows = patch_v[...].astype(F32)
    scale = lax.rsqrt(jnp.mean(rows * rows, axis=1, keepdims=True) + EPS)
    scaled = (rows * scale).astype(BF16)
    o, i = iota((256, 256), 0), iota((256, 256), 1)
    pn[...] = dot(one_hot(i == 4 * (o % 64) + o // 64), scaled).astype(BF16)

    loads[4].wait()
    acc[...] = dot(pn[0:64], up_v[0])
    gather.finish(0)
    gather.start(1)

    def up_step(p, _):
        up_part(p).wait()
        acc[...] += dot(pn[pl.ds(pl.multiple_of(64 * p, 64), 64)], up_v[p])
        return 0

    lax.fori_loop(1, 4, up_step, 0)

    h = acc[...]
    hidden = (0.5 * h * (1.0 + lax.erf(h * 0.7071067811865476))).astype(BF16)

    dest_row = dest[...].astype(F32)
    dest_col = to_column(dest_row)
    before = (iota((64, 64), 0) < iota((64, 64), 1)) & (dest_col == dest_row)
    order = jnp.sum(jnp.where(before, 1.0, 0.0), axis=0, keepdims=True)
    place = dest_row * 2.0 + order
    chosen = one_hot(iota((128, 64), 0).astype(F32) == place)
    slot_col = to_column(slot[...].astype(F32)) + 1.0
    lane = iota((64, 128), 1)
    meta = jnp.where(lane == 0, slot_col, 0.0).astype(BF16)
    doc_col = to_column(documents[...].astype(F32))
    doc_lane = (iota((256, 128), 1) - 1).astype(F32)
    counts = jnp.sum(jnp.where(doc_col == doc_lane, 1.0, 0.0), axis=0, keepdims=True)
    routed = dot(chosen, hidden).astype(BF16)
    disp[:, :, 0:1280] = routed.reshape(16, 8, 1280)
    routed_meta = (dot(chosen, meta) + counts).astype(BF16)
    disp[:, :, 1280:1408] = routed_meta.reshape(16, 8, 128)

    me_g = z * 4 + y

    def first(g, incoming):
        away = ((4 - g // 4) % 4 * 4 + (4 - g % 4) % 4) if incoming else g
        far = moved(moved(zyx, 0, away // 4), 1, away % 4)
        at = far[0] * 4 + far[1]
        return pltpu.make_async_remote_copy(
            src_ref=disp.at[at],
            dst_ref=stage1.at[at if incoming else me_g],
            send_sem=send1.at[g],
            recv_sem=recv1.at[g],
            device_id=device(far, tp),
            device_id_type=MESH,
        )

    for g in range(1, 16):
        first(g, False).start()
    stage1[me_g] = disp[me_g]
    gather.forward(1)
    for g in range(1, 16):
        first(g, True).wait_recv()
    o, i = iota((128, 128), 0), iota((128, 128), 1)
    turn = one_hot(i == ((o % 32) // 2) * 8 + (o // 32) * 2 + o % 2)
    turned[...] = dot(turn, stage1[...].reshape(128, 1408)).astype(BF16).reshape(4, 32, 1408)

    def second(g, incoming):
        far = moved(zyx, 2, -g if incoming else g)
        return pltpu.make_async_remote_copy(
            src_ref=turned.at[far[2]],
            dst_ref=stage2.at[far[2] if incoming else x],
            send_sem=send2.at[g],
            recv_sem=recv2.at[g],
            device_id=device(far, tp),
            device_id_type=MESH,
        )

    for g in range(1, 4):
        second(g, False).start()
    stage2[x] = turned[x]
    gather.finish(1)
    gather.start(2, (0, 1), True)
    gather.start(2, (2,))
    gather.forward(2, (0, 1), True)
    gather.start(2, (0, 1))
    for g in range(1, 4):
        second(g, True).wait_recv()

    arrived = stage2[...].reshape(128, 1408)
    rows_in = arrived[:, 0:1280]
    meta_in = arrived[:, 1280:1408].astype(F32)
    loads[8].wait()

    def swap(piece):
        cols = pl.ds(896 * piece, 896)
        return pltpu.make_async_remote_copy(
            src_ref=part_s.at[:, cols],
            dst_ref=part_r.at[:, cols],
            send_sem=send3.at[piece],
            recv_sem=recv3.at[piece],
            device_id=(seq, 1 - tp),
            device_id_type=MESH,
        )

    for piece in range(4):
        cols = slice(896 * piece, 896 * piece + 896)
        partial = dot(rows_in, down_v[:, cols])
        part_f[:, cols] = partial
        part_s[:, cols] = partial.astype(BF16)
        swap(piece).start()

    totals = jnp.sum(meta_in, axis=0, keepdims=True) * 0.5
    smaller = (doc_lane < doc_col) & (doc_lane >= 0.0)
    start_col = jnp.sum(jnp.where(smaller, totals, 0.0), axis=1, keepdims=True)
    total_col = to_column(totals)
    sub, lane = iota((128, 128), 0) - 1, iota((128, 128), 1)
    low = jnp.sum(jnp.where((sub >= 0) & (sub < lane), total_col, 0.0), axis=0, keepdims=True)
    high = jnp.sum(jnp.where((sub >= 0) & (sub <= lane), total_col, 0.0), axis=0, keepdims=True)
    lane = iota((1, 128), 1)
    shard_low = ((lane - 8) * 256).astype(F32)
    low = jnp.where(lane < 8, low, jnp.where(lane < 72, shard_low, -1e9))
    high = jnp.where(
        lane < 8, high, jnp.where(lane < 72, shard_low + 256.0, jnp.where(lane == 72, 0.0, -1e9))
    )
    bounds[0:1, :] = low
    bounds[1:2, :] = high

    slot_row = to_row(meta_in[:, 0:1])
    spot = (iota((256, 128), 0) + 1).astype(F32) == slot_row
    placed = one_hot(spot)
    hit = jnp.sum(jnp.where(spot, 1.0, 0.0), axis=1, keepdims=True) > 0.5
    loads[9].wait()
    squares = jnp.zeros((256, 1), F32)
    for piece in range(4):
        cols = slice(896 * piece, 896 * piece + 896)
        swap(piece).wait_recv()
        merged[...] = (part_f[:, cols] + part_r[:, cols].astype(F32)).astype(BF16)
        layer = jnp.where(hit, dot(placed, merged[...]), text_v[:, cols].astype(F32))
        text_v[:, cols] = layer.astype(BF16)
        squares += jnp.sum(layer * layer, axis=1, keepdims=True)
    out = pltpu.make_async_copy(
        text_v.at[:, pl.ds(pl.multiple_of(tp * 1792, 128), 1792)], layer_out, load.at[10]
    )
    out.start()
    factor = lax.rsqrt(squares * (1.0 / 3584.0) + EPS)
    for piece in range(4):
        cols = slice(896 * piece, 896 * piece + 896)
        normed[:, cols] = (text_v[:, cols].astype(F32) * factor).astype(BF16)

    pair = iota((256, 128), 1) % 64
    inverse = jnp.exp(pair.astype(F32) * (-2.0 / 128.0 * 13.815510557964274))
    at_t = to_column(positions[0:1, :].astype(F32))
    at_h = to_column(positions[1:2, :].astype(F32))
    at_w = to_column(positions[2:3, :].astype(F32))
    coord = jnp.where(pair < 16, at_t, jnp.where(pair < 40, at_h, at_w))
    angle = coord * inverse
    cosine = jnp.cos(angle)
    sine = jnp.sin(angle)
    sine = jnp.where(iota((256, 128), 1) < 64, -sine, sine)

    def rotated(v):
        return v * cosine + pltpu.roll(v, 64, 1) * sine

    def weight(begin, size):
        return weights[:, :, :, :, begin : begin + size].reshape(3584, size)

    gather.finish(2, (0, 1), True)
    pair = jnp.concatenate([weight(256, 128), weight(640, 128)], axis=1)
    qkv[:, 0:256] = dot(normed[...], pair)
    kv[z, y, x, :, 0:128] = rotated(qkv[:, 0:128]).astype(BF16)
    kv[z, y, x, :, 128:256] = qkv[:, 128:256].astype(BF16)
    ring.start(0)
    gather.forward(2)
    wide = iota((256, 128), 1)
    shard = wide - 8
    hidden_doc = (wide < 8) & (wide.astype(F32) != doc_col)
    hidden_shard = (wide >= 8) & ((shard >= seq) | (shard < seq - WINDOW))
    veil = jnp.where(hidden_doc | hidden_shard, MASKED, 0.0).astype(BF16)
    for head in range(7):
        query[head, :, 128:256] = veil
    unit_v[:, 128:256] = jnp.ones((UNIT, 128), BF16)
    ring.finish(0)
    ring.start(1)
    ring.forward(1)
    gather.finish(2)
    for begin, size, head in ((0, 256, 0), (384, 256, 2), (768, 384, 4)):
        qkv[:, 0:size] = dot(normed[...], weight(begin, size))
        for part in range(size // 128):
            v = qkv[:, 128 * part : 128 * part + 128]
            query[head + part, :, 0:128] = rotated(v).astype(BF16)

    ones = jnp.ones((256, 128), BF16)
    keys = kv[z, y, x, :, 0:128]
    values = jnp.concatenate([kv[z, y, x, :, 128:256], ones], axis=1)
    key_at = (iota((256, 256), 1) + seq * 256).astype(F32)
    allowed = (iota((256, 256), 1) <= iota((256, 256), 0)) & (key_at >= start_col)
    for head in range(7):
        scores = lax.dot_general(
            query[head, :, 0:128], keys, (((1,), (1,)), ((), ())), preferred_element_type=F32
        )
        scores = jnp.where(allowed, scores, MASKED)
        peak = jnp.max(scores, axis=1, keepdims=True)
        top[head] = jnp.broadcast_to(peak, (256, 128))
        hold[head] = dot(jnp.exp2((scores - peak) * EXPONENT).astype(BF16), values)

    def attend(keys, values):
        def score(head):
            return lax.dot_general(
                query[head], keys, (((1,), (1,)), ((), ())), preferred_element_type=F32
            )

        scores = score(0)
        for head in range(7):
            following = score(head + 1) if head < 6 else None
            old = top[head]
            new = jnp.maximum(old, jnp.max(scores, axis=1, keepdims=True))
            probs = jnp.exp2((scores - new[:, 0:1]) * EXPONENT).astype(BF16)
            factor = jnp.exp2((old - new) * EXPONENT)
            top[head] = new
            sums = dot(probs, values)
            hold[head, :, 0:128] = hold[head, :, 0:128] * factor + sums[:, 0:128]
            hold[head, :, 128:256] = hold[head, :, 128:256] * factor + sums[:, 128:256]
            scores = following

    def marks(first_at, rows):
        at = (iota((rows, 128), 0) + first_at).astype(F32)
        return one_hot((at >= bounds[0:1, :]) & (at < bounds[1:2, :]))

    ring.finish(1)
    ring.start(2)

    def before_unit(number):
        if number == 1:
            ring.forward(2, (0, 1))
        elif number == 2:
            ring.wait((1, 2, 1), (1, 2, 4), (0, 2, 1))
            ring.forward(2, (2,))
        elif number == 4:
            ring.wait((1, 2, 2), (1, 2, 5), (2, 2, 2), (2, 2, 5))
        elif number == 5:
            ring.wait((0, 2, 2), (0, 2, 5))

    def fill(pieces):
        at = 0
        for (row, col, begin), first_at, rows in pieces:
            here = slice(at, at + rows)
            unit_k[here, 0:128] = ring.flat[row, col, begin : begin + rows, 0:128]
            unit_v[here, 0:128] = ring.flat[row, col, begin : begin + rows, 128:256]
            unit_k[here, 128:256] = marks(first_at, rows)
            at += rows

    units = ring.units()

    def unit(number, _):
        for which, pieces in enumerate(units):

            @pl.when(number == which)
            def _():
                before_unit(which)
                fill(pieces)

        attend(unit_k[...], unit_v[...])
        return 0

    lax.fori_loop(0, len(units), unit, 0)

    @pl.when(ring.takes_extra)
    def _():
        ring.extra_copy(True).wait_recv()
        keys = jnp.concatenate(
            [extra[:, 0:128], marks((seq - WINDOW) * 256, 256)], axis=1
        )
        attend(keys, jnp.concatenate([extra[:, 128:256], ones], axis=1))

    for head in range(7):
        attended_out[:, 128 * head : 128 * head + 128] = (
            hold[head, :, 0:128] / hold[head, :, 128:256]
        ).astype(BF16)

    out.wait()
    gather.drain()
    ring.drain()
    for g in range(1, 16):
        first(g, False).wait_send()
    for g in range(1, 4):
        second(g, False).wait_send()
    for piece in range(4):
        swap(piece).wait_send()


def per_device(
    patches, merge_up, merge_down, dest, slot, text, positions, documents, w_query, w_key, w_value
):
    hbm = pl.BlockSpec(memory_space=pl.ANY)
    vmem = pl.BlockSpec(memory_space=pltpu.VMEM)
    dma = pltpu.SemaphoreType.DMA
    return pl.pallas_call(
        whole,
        out_shape=(
            jax.ShapeDtypeStruct((256, 1792), BF16),
            jax.ShapeDtypeStruct((256, 896), BF16),
        ),
        in_specs=[hbm, hbm, hbm, vmem, vmem, hbm, vmem, vmem, hbm, hbm, hbm],
        out_specs=(hbm, vmem),
        scratch_shapes=[
            pltpu.VMEM((256, 1280), BF16),
            pltpu.VMEM((4, 1280, 1280), BF16),
            pltpu.VMEM((1280, 3584), BF16),
            pltpu.VMEM((256, 3584), BF16),
            pltpu.VMEM((256, 1280), BF16),
            pltpu.VMEM((64, 1280), F32),
            pltpu.VMEM((16, 8, 1408), BF16),
            pltpu.VMEM((16, 8, 1408), BF16),
            pltpu.VMEM((4, 32, 1408), BF16),
            pltpu.VMEM((4, 32, 1408), BF16),
            pltpu.VMEM((128, 3584), F32),
            pltpu.VMEM((128, 3584), BF16),
            pltpu.VMEM((128, 3584), BF16),
            pltpu.VMEM((128, 896), BF16),
            pltpu.VMEM((256, 3584), BF16),
            pltpu.VMEM((4, 4, 4, 56, 1152), BF16),
            pltpu.VMEM((256, 384), F32),
            pltpu.VMEM((4, 4, 4, 256, 256), BF16),
            pltpu.VMEM((256, 256), BF16),
            pltpu.VMEM((8, 128), F32),
            pltpu.VMEM((7, 256, 256), BF16),
            pltpu.VMEM((7, 256, 256), F32),
            pltpu.VMEM((7, 256, 128), F32),
            pltpu.VMEM((UNIT, 256), BF16),
            pltpu.VMEM((UNIT, 256), BF16),
            dma((13,)),
            dma((66,)),
            dma((66,)),
            dma((16,)),
            dma((16,)),
            dma((4,)),
            dma((4,)),
            dma((4,)),
            dma((4,)),
            dma((55,)),
            dma((55,)),
        ],
        compiler_params=pltpu.CompilerParams(
            collective_id=0, has_side_effects=True, vmem_limit_bytes=67043328
        ),
        name="whole",
    )(
        patches, merge_up, merge_down, dest.reshape(1, -1), slot.reshape(1, -1), text, positions,
        documents.reshape(1, -1), w_query, w_key, w_value,
    )


def solution(mesh):
    in_specs = (
        P("seq", None),
        P(None, "tp"),
        P("tp", None),
        P("seq"),
        P("seq"),
        P("seq", None),
        P(None, "seq"),
        P("seq"),
        P("seq", "tp"),
        P("seq", "tp"),
        P("seq", "tp"),
    )
    out_specs = (P("seq", "tp"), P("seq", "tp"))
    return jax.shard_map(
        per_device, mesh=mesh, in_specs=in_specs, out_specs=out_specs, check_vma=False
    )
```

profile of v0, /device:TPU:96, one launch (start us, length us, event | category | flops | bytes accessed | tf_op | source)
XLA Modules:
  0.0 97.4 jit_solution(7700196488738765818)
XLA Ops:
  0.6 92.8 %whole.1 = (bf16[256,1792]{1,0:T(8,128)(2,1)}, bf16[256,896]{1,0:T(8,128)(2,1)}) custom-call(bf16[256,1280]{1,0:T(8,128)(2,1)} %patches.1, bf16[5120,1280]{1,0:T(8,128)(2,1)} %merge_up.1, bf16[1280,3584]{1,0:T(8,128)(2,1)} %merge_down.1, s32[1,64]{1,0:T(1,128)} %bitcast.4, s32[1,64]{1,0:T(1,128)} %bitcast.5, bf16[256,3584]{1,0:T(8,128)(2,1)} %text.1, ...), custom_call_target="tpu_custom_call" | custom-call | tf_op jit(solution)/shard_map/whole/pallas_call | solution.py:669
  93.4 2.2 %copy.15 = bf16[256,1792]{1,0:T(8,128)(2,1)} copy(bf16[256,1792]{1,0:T(8,128)(2,1)} %get-tuple-element.4) | data formatting | bytes 1835008
  95.6 1.8 %copy.16 = bf16[256,896]{1,0:T(8,128)(2,1)} copy(bf16[256,896]{1,0:T(8,128)(2,1)} %get-tuple-element.5) | data formatting | bytes 917504
where the time goes:
time: 97.6 us; the launch traced here: 97.4 us
  Pallas kernels  92.8 us (95%)
  local copies, waits for them, and re-layouts  3.98 us (4%)
    pallas_call x1, Pallas kernels, per_device(): pl.pallas_call(whole, out_shape=(jax.ShapeDtypeStruct((256, 1792), BF16),...  92.8 us
    unnamed x2, local copies, waits for them, and re-layouts  3.98 us

commit v1 on v0

--- a/solution.py
+++ b/solution.py
@@ -34,73 +34,93 @@
     return tuple(out)
 
 
+def bulk(ref, send_sem, recv_sem, seq, tp):
+    return pltpu.make_async_remote_copy(
+        src_ref=ref, dst_ref=ref, send_sem=send_sem, recv_sem=recv_sem,
+        device_id=(seq, 1 - tp), device_id_type=MESH,
+    )
+
+
 class Gather:
     ORDERS = ((2, 1, 0), (1, 0, 2), (0, 2, 1))
 
-    def __init__(self, weights, send, recv, zyx, tp):
+    def __init__(self, weights, send, recv, zyx, tp, seq):
         self.weights, self.send, self.recv, self.zyx, self.tp = weights, send, recv, zyx, tp
-
-    def block(self, part, phase, at, half, early):
-        order = self.ORDERS[part]
-        index = [None, None, None]
-        for place, dim in enumerate(order):
-            if place < phase:
-                index[dim] = pl.ds(0, 4)
-            elif place == phase:
-                index[dim] = at
-            else:
-                index[dim] = self.zyx[dim]
-        if phase:
-            index[order[phase - 1]] = pl.ds(2 * half, 2)
-        columns = pl.ds(384 * part, 384)
-        if phase == 2 and part < 2:
-            columns = pl.ds(384 * part + 256, 128) if early else pl.ds(384 * part, 256)
-        return self.weights.at[index[0], index[1], index[2], :, columns]
-
-    def copy(self, part, phase, kind, incoming=False, early=False):
-        dim = self.ORDERS[part][phase]
-        me = self.zyx[dim]
-        back, half = ((0, 0), (0, 1), (1, 0), (0, 1), (0, 0), (1, 1))[kind]
-        step = 1 if kind < 3 else -1
-        if phase == 0 and kind == 2:
-            back, step = 0, 2
-        shift = (1 if kind < 3 else -1) * back + (step if incoming else 0)
-        at = lax.rem(me - shift + 4, 4)
-        ref = self.block(part, phase, at, half, early)
-        sem = 54 + part * 6 + kind if early else (part * 3 + phase) * 6 + kind
+        self.seq = seq
+
+    def bulk(self, ref, send, recv):
+        return bulk(ref, self.send.at[send], self.recv.at[recv], self.seq, self.tp)
+
+    def make(self, part, dim, step, index, columns, phase, sem):
+        index = tuple(index)
+        ref = self.weights.at[index[0], index[1], index[2], :, pl.ds(*columns)]
         return pltpu.make_async_remote_copy(
             src_ref=ref,
             dst_ref=ref,
-            send_sem=self.send.at[sem],
+            send_sem=self.send.at[phase],
             recv_sem=self.recv.at[sem],
             device_id=device(moved(self.zyx, dim, step), self.tp),
             device_id_type=MESH,
         )
 
-    def start(self, phase, parts=(0, 1, 2), early=False):
-        for kind in (0, 3, 2) if phase == 0 else (0, 3, 1, 4):
+    def own(self, part, which, incoming=False):
+        dim = self.ORDERS[part][0]
+        step = (1, -1, 2)[which]
+        index = list(self.zyx)
+        index[dim] = lax.rem(index[dim] - (step if incoming else 0) + 4, 4)
+        return self.make(part, dim, step, index, (384 * part, 384), 0, 0)
+
+    def copy(self, part, phase, sign, piece, forwarded=False, incoming=False, early=False):
+        order = self.ORDERS[part]
+        dim = order[phase]
+        index = list(self.zyx)
+        if phase == 2:
+            index[order[0]] = pl.ds(0, 4)
+        before = order[phase - 1]
+        index[before] = lax.rem(self.zyx[before] + piece, 4)
+        back = sign * ((1 if forwarded else 0) + (1 if incoming else 0))
+        index[dim] = lax.rem(self.zyx[dim] - back + 4, 4)
+        columns = (384 * part, 384)
+        if phase == 2 and part < 2:
+            columns = (384 * part + 256, 128) if early else (384 * part, 256)
+        group = 2 if early else phase - 1
+        sem = 33 + group
+        if not forwarded and sign == (1 if piece < 2 else -1):
+            sem = 1 + 12 * group + 4 * part + piece
+        return self.make(part, dim, sign, index, columns, phase, sem)
+
+    def start_own(self):
+        for which in range(3):
+            for part in range(3):
+                self.own(part, which).start()
+
+    def finish_own(self):
+        self.bulk(self.weights.at[0, 0, pl.ds(0, 3)], 0, 0).wait_recv()
+
+    def start(self, phase, pieces, parts=(0, 1, 2), early=False):
+        for piece in pieces:
             for part in parts:
-                self.copy(part, phase, kind, early=early).start()
-
-    def forward(self, phase, parts=(0, 1, 2), early=False):
-        for kind in (2, 5):
+                for sign in (1, -1):
+                    self.copy(part, phase, sign, piece, early=early).start()
+
+    def forward(self, phase, pieces, parts=(0, 1, 2), early=False):
+        for piece in pieces:
+            sign = 1 if piece < 2 else -1
             for part in parts:
-                self.copy(part, phase, kind - 2, True, early).wait_recv()
-                self.copy(part, phase, kind, early=early).start()
-
-    def finish(self, phase, parts=(0, 1, 2), early=False):
-        for part in parts:
-            for kind in (0, 3, 2) if phase == 0 else (1, 4, 2, 5):
-                self.copy(part, phase, kind, True, early).wait_recv()
+                self.copy(part, phase, sign, piece, incoming=True, early=early).wait_recv()
+                self.copy(part, phase, sign, piece, forwarded=True, early=early).start()
+
+    def finish(self, phase, early=False):
+        if phase == 1:
+            ref = self.weights.at[0, pl.ds(0, 2)]
+        else:
+            ref = self.weights.at[pl.ds(0, 2), :, :, :, pl.ds(0, 256 if early else 896)]
+        self.bulk(ref, phase, 35 if early else 32 + phase).wait_recv()
 
     def drain(self):
-        for phase in range(3):
-            for part in range(3):
-                for kind in (0, 3, 2) if phase == 0 else range(6):
-                    self.copy(part, phase, kind).wait_send()
-        for part in range(2):
-            for kind in range(6):
-                self.copy(part, 2, kind, early=True).wait_send()
+        self.bulk(self.weights.at[0, 0, pl.ds(0, 3)], 0, 0).wait_send()
+        self.bulk(self.weights.at[0, pl.ds(0, 3)], 1, 0).wait_send()
+        self.bulk(self.weights.at[pl.ds(0, 3)], 2, 0).wait_send()
 
 
 class Ring:
@@ -160,11 +180,18 @@
             ref = self.kv.at[planes, at, :, pl.ds(*self.PARTS[2])]
         else:
             ref = self.block(part, phase, at, kind)
-        sem = (part * 3 + phase) * 6 + kind
+        if phase == 0:
+            sends, sem = 0, 0
+        elif phase == 1:
+            sends, sem = 1 + part, 7 + part
+            if kind in (0, 3):
+                sem = 1 + 2 * part + kind // 3
+        else:
+            sends, sem = 4 + part, 10 + 6 * part + kind
         return pltpu.make_async_remote_copy(
             src_ref=ref,
             dst_ref=ref,
-            send_sem=self.send.at[sem],
+            send_sem=self.send.at[sends],
             recv_sem=self.recv.at[sem],
             device_id=device(moved(self.zyx, dim, sign), self.tp),
             device_id_type=MESH,
@@ -204,17 +231,24 @@
                 self.wait((part, phase, kind - 2))
                 self.copy(part, phase, kind).start()
 
+    def bulk(self, rows, cols, part, send, recv):
+        tokens = pl.ds(0, 256 if part is None else self.PARTS[part][1])
+        ref = self.flat.at[pl.ds(0, rows), pl.ds(0, cols), tokens]
+        return bulk(ref, self.send.at[send], self.recv.at[recv], self.seq, self.tp)
+
     def finish(self, phase):
+        if phase == 0:
+            self.bulk(1, 3, None, 0, 0).wait_recv()
+            return
         for part in range(3):
-            for kind in self.own_kinds(part, phase) + self.sent_on(phase):
-                if phase == 0 or kind not in (0, 3):
-                    self.wait((part, phase, kind))
+            self.bulk(2, 3 if part == 2 else 4, part, 1 + part, 7 + part).wait_recv()
 
     def drain(self):
-        for phase in range(3):
-            for part in range(3):
-                for kind in self.own_kinds(part, phase) + self.sent_on(phase):
-                    self.copy(part, phase, kind).wait_send()
+        self.bulk(1, 3, None, 0, 0).wait_send()
+        for part, (rows, cols) in enumerate(((3, 4), (3, 4), (3, 3))):
+            self.bulk(rows, cols, part, 1 + part, 0).wait_send()
+        for part, (rows, cols) in enumerate(((10, 4), (9, 3), (6, 4))):
+            self.bulk(rows, cols, part, 4 + part, 0).wait_send()
 
         @pl.when(self.gives_extra)
         def _():
@@ -223,12 +257,11 @@
     def extra_copy(self, incoming):
         z, y, x = self.zyx
         other = (self.seq + 64 - WINDOW if incoming else self.seq + WINDOW) % 64
-        sem = 54
         return pltpu.make_async_remote_copy(
             src_ref=self.kv.at[z, y, x],
             dst_ref=self.extra,
-            send_sem=self.send.at[sem],
-            recv_sem=self.recv.at[sem],
+            send_sem=self.send.at[7],
+            recv_sem=self.recv.at[28],
             device_id=(other, self.tp),
             device_id_type=MESH,
         )
@@ -367,11 +400,6 @@
     ring.greet(barrier)
     for copy in own_loads:
         copy.wait()
-    ring.greeted(barrier, len(partners))
-
-    gather = Gather(weights, send, recv, zyx, tp)
-    gather.start(0)
-
     loads[3].wait()
     rows = patch_v[...].astype(F32)
     scale = lax.rsqrt(jnp.mean(rows * rows, axis=1, keepdims=True) + EPS)
@@ -379,10 +407,16 @@
     o, i = iota((256, 256), 0), iota((256, 256), 1)
     pn[...] = dot(one_hot(i == 4 * (o % 64) + o // 64), scaled).astype(BF16)
 
+    ring.greeted(barrier, len(partners))
+
+    gather = Gather(weights, send, recv, zyx, tp, seq)
+    gather.start_own()
+    gather.start(1, (0,))
+
     loads[4].wait()
     acc[...] = dot(pn[0:64], up_v[0])
-    gather.finish(0)
-    gather.start(1)
+    gather.finish_own()
+    gather.start(1, (3, 1, 2))
 
     def up_step(p, _):
         up_part(p).wait()
@@ -413,50 +447,51 @@
 
     me_g = z * 4 + y
 
-    def first(g, incoming):
-        away = ((4 - g // 4) % 4 * 4 + (4 - g % 4) % 4) if incoming else g
-        far = moved(moved(zyx, 0, away // 4), 1, away % 4)
+    def first(g):
+        far = moved(moved(zyx, 0, g // 4), 1, g % 4)
         at = far[0] * 4 + far[1]
         return pltpu.make_async_remote_copy(
             src_ref=disp.at[at],
-            dst_ref=stage1.at[at if incoming else me_g],
-            send_sem=send1.at[g],
-            recv_sem=recv1.at[g],
+            dst_ref=stage1.at[me_g],
+            send_sem=send1.at[0],
+            recv_sem=recv1.at[0],
             device_id=device(far, tp),
             device_id_type=MESH,
         )
 
     for g in range(1, 16):
-        first(g, False).start()
+        first(g).start()
     stage1[me_g] = disp[me_g]
-    gather.forward(1)
-    for g in range(1, 16):
-        first(g, True).wait_recv()
+    gather.forward(1, (0, 3, 1, 2))
+    gather.start(2, (0,), (0, 1), True)
+    gather.start(2, (0,))
+    bulk(stage1.at[pl.ds(0, 15)], send1.at[0], recv1.at[0], seq, tp).wait_recv()
     o, i = iota((128, 128), 0), iota((128, 128), 1)
     turn = one_hot(i == ((o % 32) // 2) * 8 + (o // 32) * 2 + o % 2)
     turned[...] = dot(turn, stage1[...].reshape(128, 1408)).astype(BF16).reshape(4, 32, 1408)
 
-    def second(g, incoming):
-        far = moved(zyx, 2, -g if incoming else g)
+    def second(g):
+        far = moved(zyx, 2, g)
         return pltpu.make_async_remote_copy(
             src_ref=turned.at[far[2]],
-            dst_ref=stage2.at[far[2] if incoming else x],
-            send_sem=send2.at[g],
-            recv_sem=recv2.at[g],
+            dst_ref=stage2.at[x],
+            send_sem=send2.at[0],
+            recv_sem=recv2.at[0],
             device_id=device(far, tp),
             device_id_type=MESH,
         )
 
     for g in range(1, 4):
-        second(g, False).start()
+        second(g).start()
     stage2[x] = turned[x]
+    gather.forward(2, (0,), (0, 1), True)
     gather.finish(1)
-    gather.start(2, (0, 1), True)
-    gather.start(2, (2,))
-    gather.forward(2, (0, 1), True)
-    gather.start(2, (0, 1))
-    for g in range(1, 4):
-        second(g, True).wait_recv()
+    gather.start(2, (3, 2, 1), (0, 1), True)
+    gather.start(2, (3, 2, 1), (2,))
+    gather.start(2, (3,), (0, 1))
+    bulk(stage2.at[pl.ds(0, 3)], send2.at[0], recv2.at[0], seq, tp).wait_recv()
+    gather.forward(2, (3, 2, 1), (0, 1), True)
+    gather.start(2, (2, 1), (0, 1))
 
     arrived = stage2[...].reshape(128, 1408)
     rows_in = arrived[:, 0:1280]
@@ -468,7 +503,7 @@
         return pltpu.make_async_remote_copy(
             src_ref=part_s.at[:, cols],
             dst_ref=part_r.at[:, cols],
-            send_sem=send3.at[piece],
+            send_sem=send3.at[0],
             recv_sem=recv3.at[piece],
             device_id=(seq, 1 - tp),
             device_id_type=MESH,
@@ -536,13 +571,13 @@
     def weight(begin, size):
         return weights[:, :, :, :, begin : begin + size].reshape(3584, size)
 
-    gather.finish(2, (0, 1), True)
+    gather.finish(2, True)
     pair = jnp.concatenate([weight(256, 128), weight(640, 128)], axis=1)
     qkv[:, 0:256] = dot(normed[...], pair)
     kv[z, y, x, :, 0:128] = rotated(qkv[:, 0:128]).astype(BF16)
     kv[z, y, x, :, 128:256] = qkv[:, 128:256].astype(BF16)
     ring.start(0)
-    gather.forward(2)
+    gather.forward(2, (0, 3, 2, 1))
     wide = iota((256, 128), 1)
     shard = wide - 8
     hidden_doc = (wide < 8) & (wide.astype(F32) != doc_col)
@@ -652,12 +687,32 @@
     out.wait()
     gather.drain()
     ring.drain()
-    for g in range(1, 16):
-        first(g, False).wait_send()
-    for g in range(1, 4):
-        second(g, False).wait_send()
-    for piece in range(4):
-        swap(piece).wait_send()
+    bulk(stage1.at[pl.ds(0, 15)], send1.at[0], recv1.at[0], seq, tp).wait_send()
+    bulk(stage2.at[pl.ds(0, 3)], send2.at[0], recv2.at[0], seq, tp).wait_send()
+    bulk(part_s, send3.at[0], recv3.at[0], seq, tp).wait_send()
+
+
+def hand_over(layer, attended, layer_out, attended_out, layer_v, attended_v, into, out):
+    moves = []
+    for n in range(4):
+        moves.append((layer, layer_v, layer_out, pl.ds(64 * n, 64)))
+    for n in range(2):
+        moves.append((attended, attended_v, attended_out, pl.ds(128 * n, 128)))
+    first = [
+        pltpu.make_async_copy(a.at[rows], b.at[rows], into.at[n])
+        for n, (a, b, _, rows) in enumerate(moves)
+    ]
+    then = [
+        pltpu.make_async_copy(b.at[rows], c.at[rows], out.at[n])
+        for n, (_, b, c, rows) in enumerate(moves)
+    ]
+    for copy in first:
+        copy.start()
+    for arrives, leaves in zip(first, then):
+        arrives.wait()
+        leaves.start()
+    for copy in then:
+        copy.wait()
 
 
 def per_device(
@@ -666,7 +721,7 @@
     hbm = pl.BlockSpec(memory_space=pl.ANY)
     vmem = pl.BlockSpec(memory_space=pltpu.VMEM)
     dma = pltpu.SemaphoreType.DMA
-    return pl.pallas_call(
+    layer_part, attended = pl.pallas_call(
         whole,
         out_shape=(
             jax.ShapeDtypeStruct((256, 1792), BF16),
@@ -701,16 +756,16 @@
             pltpu.VMEM((UNIT, 256), BF16),
             pltpu.VMEM((UNIT, 256), BF16),
             dma((13,)),
-            dma((66,)),
-            dma((66,)),
-            dma((16,)),
-            dma((16,)),
+            dma((3,)),
+            dma((36,)),
+            dma((1,)),
+            dma((1,)),
+            dma((1,)),
+            dma((1,)),
+            dma((1,)),
             dma((4,)),
-            dma((4,)),
-            dma((4,)),
-            dma((4,)),
-            dma((55,)),
-            dma((55,)),
+            dma((8,)),
+            dma((29,)),
         ],
         compiler_params=pltpu.CompilerParams(
             collective_id=0, has_side_effects=True, vmem_limit_bytes=67043328
@@ -720,6 +775,22 @@
         patches, merge_up, merge_down, dest.reshape(1, -1), slot.reshape(1, -1), text, positions,
         documents.reshape(1, -1), w_query, w_key, w_value,
     )
+    return pl.pallas_call(
+        hand_over,
+        out_shape=(
+            jax.ShapeDtypeStruct((256, 1792), BF16),
+            jax.ShapeDtypeStruct((256, 896), BF16),
+        ),
+        in_specs=[hbm, hbm],
+        out_specs=(hbm, hbm),
+        scratch_shapes=[
+            pltpu.VMEM((256, 1792), BF16),
+            pltpu.VMEM((256, 896), BF16),
+            dma((6,)),
+            dma((6,)),
+        ],
+        name="hand_over",
+    )(layer_part, attended)
 
 
 def solution(mesh):

time: 97.6 us -> 92.4 us (0.947)
  local copies, waits for them, and re-layouts: 3.98 us -> 0 us
  Pallas kernels: 92.8 us -> 90.7 us
    pallas_call x1, Pallas kernels: 92.8 us -> 88.5 us  [per_device(): pl.pallas_call(whole, out_shape=(jax.ShapeDtypeStruct((256, 1792), BF16),...]
    unnamed x2 -> x0, local copies, waits for them, and re-layouts: 3.98 us -> none
    pallas_call x0 -> x1, Pallas kernels: none -> 2.22 us  [per_device(): pl.pallas_call(hand_over, out_shape=(jax.ShapeDtypeStruct((256, 1792), BF...]
where the time goes in v1:
time: 92.4 us; the launch traced here: 91.5 us
  Pallas kernels  90.7 us (98%)
    pallas_call x1, Pallas kernels, per_device(): pl.pallas_call(whole, out_shape=(jax.ShapeDtypeStruct((256, 1792), BF16),...  88.5 us
    pallas_call x1, Pallas kernels, per_device(): pl.pallas_call(hand_over, out_shape=(jax.ShapeDtypeStruct((256, 1792), BF...  2.22 us

profile of v1, /device:TPU:96, one launch (start us, length us, event | category | flops | bytes accessed | tf_op | source)
XLA Modules:
  0.0 91.5 jit_solution(7571777149856219885)
XLA Ops:
  0.6 88.5 %whole.1 = (bf16[256,1792]{1,0:T(8,128)(2,1)}, bf16[256,896]{1,0:T(8,128)(2,1)}) custom-call(bf16[256,1280]{1,0:T(8,128)(2,1)} %patches.1, bf16[5120,1280]{1,0:T(8,128)(2,1)} %merge_up.1, bf16[1280,3584]{1,0:T(8,128)(2,1)} %merge_down.1, s32[1,64]{1,0:T(1,128)} %bitcast.4, s32[1,64]{1,0:T(1,128)} %bitcast.5, bf16[256,3584]{1,0:T(8,128)(2,1)} %text.1, ...), custom_call_target="tpu_custom_call" | custom-call | tf_op jit(solution)/shard_map/whole/pallas_call | solution.py:724
  89.1 2.2 %hand_over.1 = (bf16[256,1792]{1,0:T(8,128)(2,1)}, bf16[256,896]{1,0:T(8,128)(2,1)}) custom-call(bf16[256,1792]{1,0:T(8,128)(2,1)} %get-tuple-element.4.layer, bf16[256,896]{1,0:T(8,128)(2,1)} %get-tuple-element.5.attended), custom_call_target="tpu_custom_call" | custom-call | tf_op jit(solution)/shard_map/hand_over/pallas_call | solution.py:778

commit v2 on v1

--- a/solution.py
+++ b/solution.py
@@ -489,6 +489,7 @@
     gather.start(2, (3, 2, 1), (0, 1), True)
     gather.start(2, (3, 2, 1), (2,))
     gather.start(2, (3,), (0, 1))
+    gather.forward(2, (0,))
     bulk(stage2.at[pl.ds(0, 3)], send2.at[0], recv2.at[0], seq, tp).wait_recv()
     gather.forward(2, (3, 2, 1), (0, 1), True)
     gather.start(2, (2, 1), (0, 1))
@@ -577,7 +578,7 @@
     kv[z, y, x, :, 0:128] = rotated(qkv[:, 0:128]).astype(BF16)
     kv[z, y, x, :, 128:256] = qkv[:, 128:256].astype(BF16)
     ring.start(0)
-    gather.forward(2, (0, 3, 2, 1))
+    gather.forward(2, (3, 2, 1))
     wide = iota((256, 128), 1)
     shard = wide - 8
     hidden_doc = (wide < 8) & (wide.astype(F32) != doc_col)
@@ -658,26 +659,41 @@
 
     units = ring.units()
 
+    def from_extra(number):
+        begin, at, rows = ((1120, 0, 64), (1344, 64, 192))[number - 4]
+        here, there = slice(begin, begin + rows), slice(at, at + rows)
+        unit_k[here, 0:128] = extra[there, 0:128]
+        unit_v[here, 0:128] = extra[there, 128:256]
+        unit_k[here, 128:256] = marks((seq - WINDOW) * 256 + at, rows)
+
     def unit(number, _):
+        used = number < 0
         for which, pieces in enumerate(units):
+            for _, first_at, _ in pieces:
+                seen = (first_at >= (seq - WINDOW) * 256) & (first_at < seq * 256)
+                used = used | ((number == which) & seen)
 
             @pl.when(number == which)
             def _():
                 before_unit(which)
                 fill(pieces)
 
-        attend(unit_k[...], unit_v[...])
+        @pl.when(ring.takes_extra & (number == 4))
+        def _():
+            ring.extra_copy(True).wait_recv()
+            from_extra(4)
+
+        @pl.when(ring.takes_extra & (number == 5))
+        def _():
+            from_extra(5)
+
+        @pl.when(used)
+        def _():
+            attend(unit_k[...], unit_v[...])
+
         return 0
 
     lax.fori_loop(0, len(units), unit, 0)
-
-    @pl.when(ring.takes_extra)
-    def _():
-        ring.extra_copy(True).wait_recv()
-        keys = jnp.concatenate(
-            [extra[:, 0:128], marks((seq - WINDOW) * 256, 256)], axis=1
-        )
-        attend(keys, jnp.concatenate([extra[:, 128:256], ones], axis=1))
 
     for head in range(7):
         attended_out[:, 128 * head : 128 * head + 128] = (

time: 92.4 us -> 93.1 us (level)
  the two profiles are of different devices: /device:TPU:96 before, /device:TPU:0 now
where the time goes in v2:
time: 93.1 us; the launch traced here: 92.9 us
  Pallas kernels  92.1 us (99%)
    pallas_call x1, Pallas kernels, per_device(): pl.pallas_call(whole, out_shape=(jax.ShapeDtypeStruct((256, 1792), BF16),...  89.9 us
    pallas_call x1, Pallas kernels, per_device(): pl.pallas_call(hand_over, out_shape=(jax.ShapeDtypeStruct((256, 1792), BF...  2.22 us

profile of v2, /device:TPU:0, one launch (start us, length us, event | category | flops | bytes accessed | tf_op | source)
XLA Modules:
  0.0 92.9 jit_solution(1954449332760176991)
XLA Ops:
  0.6 89.9 %whole.1 = (bf16[256,1792]{1,0:T(8,128)(2,1)}, bf16[256,896]{1,0:T(8,128)(2,1)}) custom-call(bf16[256,1280]{1,0:T(8,128)(2,1)} %patches.1, bf16[5120,1280]{1,0:T(8,128)(2,1)} %merge_up.1, bf16[1280,3584]{1,0:T(8,128)(2,1)} %merge_down.1, s32[1,64]{1,0:T(1,128)} %bitcast.4, s32[1,64]{1,0:T(1,128)} %bitcast.5, bf16[256,3584]{1,0:T(8,128)(2,1)} %text.1, ...), custom_call_target="tpu_custom_call" | custom-call | tf_op jit(solution)/shard_map/whole/pallas_call | solution.py:740
  90.5 2.2 %hand_over.1 = (bf16[256,1792]{1,0:T(8,128)(2,1)}, bf16[256,896]{1,0:T(8,128)(2,1)}) custom-call(bf16[256,1792]{1,0:T(8,128)(2,1)} %get-tuple-element.4.layer, bf16[256,896]{1,0:T(8,128)(2,1)} %get-tuple-element.5.attended), custom_call_target="tpu_custom_call" | custom-call | tf_op jit(solution)/shard_map/hand_over/pallas_call | solution.py:794
